TPU v7x, 32 devices: a whole 2x2x4 slice. The times are simulated.
32 devices in a mesh: vert: 8 (over z, x), af: 4 (over y, core).
Axes of the slice: x: 2, y: 2, z: 4, core: 2. Of those that a mesh axis runs over, the one named last changes fastest.
Arguments:
- features_t: bfloat16 [128, 4096], P('af', 'vert'), may hold values from -24 to 24
- weight: bfloat16 [128, 256], P('af'), may hold values from -1 to 1
- bias: float32 [256], P('af'), may hold values from -3 to 3
- self_mask: int32 [8, 512, 512], P('vert'), may hold values 0 or 1
- halo_mask: int32 [8, 6, 512, 256], P('vert'), may hold values 0 or 1
- block_src: int32 [8, 6], P('vert'), may hold values from -1 to 7, as said below
- halo_rows: int32 [8, 6, 256], P('vert'), may hold values from 0 to 511, as said below
- outside_degree: int32 [4096], P('vert'), may hold values from 0 to 47
Outputs:
- output_t: bfloat16 [256, 4096], P('af', 'vert')
Inputs may be any that keep to these rules, and one draw needn't show every extreme that they name: `block_src`: the live sources of a row are distinct partitions other than the row's own; empty slots (-1) come after the live ones; every row has at least one live slot and some row has all 6. `halo_rows`: the entries of one slot are distinct.
All inputs are finite; a program needn't handle non-finite values. No bound on the sum of `self_mask` or of `halo_mask` on one device may be relied on, other than what follows from the above.
Results may differ from a plain program's by a relative error of at most 0.0054.
Values may be sent and summed in bfloat16 or wider, within the bound.
A program may use at most 64 MiB of HBM per device.

v0:
```python
import jax
import jax.numpy as jnp
from jax import lax
from jax.sharding import PartitionSpec as P


def body(features_t, weight, bias, self_mask, halo_mask, block_src, halo_rows, outside_degree):
    sources = block_src[0]
    rows = halo_rows[0]
    live_slot = sources >= 0
    block_rows = features_t.shape[1]
    feat_count = features_t.shape[0]
    live_blocks = halo_mask[0] * live_slot.astype(jnp.int32)[:, None, None]
    degree = (
        1
        + jnp.sum(self_mask[0], axis=-1)
        + jnp.sum(jnp.sum(live_blocks, axis=-1), axis=0)
        + outside_degree
    )
    inverse_root = 1.0 / jnp.sqrt(degree.astype(jnp.float32))
    scaled = (features_t.astype(jnp.float32) * inverse_root[None, :]).astype(jnp.bfloat16)
    own_mask = self_mask[0].astype(jnp.bfloat16)
    summed_rows = scaled.astype(jnp.float32) + lax.dot_general(
        scaled, own_mask, (((1,), (1,)), ((), ())), preferred_element_type=jnp.float32
    )
    safe_sources = jnp.maximum(sources, 0)
    gathered = lax.all_gather(scaled, "vert", axis=1, tiled=True)
    column_ids = (safe_sources * block_rows)[:, None] + rows
    halo_vals = jnp.take(gathered, column_ids.reshape(-1), axis=1).reshape(
        feat_count, rows.shape[0], rows.shape[1]
    )
    halo_blocks = live_blocks.astype(jnp.bfloat16)
    summed_rows = summed_rows + jnp.einsum(
        "fsk,sik->fi", halo_vals, halo_blocks, preferred_element_type=jnp.float32
    )
    aggregated = (summed_rows * inverse_root[None, :]).astype(jnp.bfloat16)
    out_rows = bias.shape[0]
    all_inputs, all_weight = (
        lax.all_gather(aggregated, "af", axis=0, tiled=True),
        lax.all_gather(weight, "af", axis=0, tiled=True),
    )
    first_col = lax.axis_index("af") * out_rows
    weight_cols = lax.dynamic_slice_in_dim(all_weight, first_col, out_rows, 1)
    mixed = lax.dot_general(
        weight_cols, all_inputs, (((0,), (0,)), ((), ())), preferred_element_type=jnp.float32
    )
    return jnp.maximum(mixed + bias[:, None], 0.0).astype(jnp.bfloat16)


def solution(mesh):
    return jax.shard_map(
        body,
        mesh=mesh,
        in_specs=(
            P("af", "vert"),
            P("af", None),
            P("af"),
            P("vert", None, None),
            P("vert", None, None, None),
            P("vert", None),
            P("vert", None, None),
            P("vert"),
        ),
        out_specs=P("af", "vert"),
        check_vma=False,
    )
```

profile of v0, /device:TPU:0, one launch (start us, length us, event | category | flops | bytes accessed | tf_op | source)
XLA Modules:
  0.0 60.5 jit_solution(17905522223781687085)
XLA Ops:
  0.0 0.0 copy-start.7
  0.0 0.0 copy-start.5
  0.0 0.0 copy-start.2
  0.0 0.0 copy-start.3
  0.0 0.7 %fusion.20 = s32[6]{0:T(128)S(1)} fusion(s32[1,6]{1,0:T(1,128)} %param.13), kind=kLoop, calls=%fused_computation.30 | loop fusion | flops 12 | bytes 48 | tf_op jit(solution)/shard_map/convert_element_type | solution.py:13
  0.7 0.0 copy-start
  0.7 2.4 %fusion.1 = s32[512]{0:T(512)S(1)} fusion(s32[1,6,512,256]{3,2,1,0:T(8,128)} %param.12, s32[6]{0:T(128)S(1)} %fusion.20), kind=kLoop, calls=%fused_computation.3 | loop fusion | flops 1572352 | bytes 3147800 | tf_op jit(solution)/shard_map/reduce_sum | solution.py:17
  3.2 1.4 %reduce_sum.16 = s32[512]{0:T(512)S(1)} reduce(s32[1,512,512]{2,1,0:T(8,128)} %param.11, s32[]{:T(128)} %constant.10.clone.1), dimensions={0,2}, to_apply=%region_0.0 | reduce | flops 261632 | bytes 1050628 | tf_op jit(solution)/shard_map/reduce_sum | solution.py:16
  4.5 0.0 copy-done.5
  4.6 0.0 copy-done.2
  4.6 0.1 copy.10
  4.7 0.1 multiply_convert_fusion
  4.8 36.6 %all_gather.10 = bf16[32,4096]{0,1:T(8,128)(2,1)} all-gather(bf16[32,512]{0,1:T(8,128)(2,1)S(1)} %multiply_convert_fusion), channel_id=1, replica_groups=mesh['vert'=8,'af'=4] {'vert'}, dimensions={1}, use_global_device_ids=true | all-gather | bytes 294912 | tf_op jit(solution)/shard_map/all_gather | solution.py:27
  41.4 0.0 copy-done.7
  41.4 0.1 broadcast_bitcast_fusion
  41.5 0.0 copy-done.3
  41.6 0.0 copy-start.4
  41.6 0.0 copy-start.6
  41.6 5.0 %gather_fusion = bf16[1536,32]{1,0:T(8,128)(2,1)} fusion(bf16[32,4096]{0,1:T(8,128)(2,1)} %all_gather.10, s32[2048]{0:T(1024)S(1)} %pad_clamp_fusion), kind=kCustom, calls=%fused_computation | custom fusion | bytes 202752 | tf_op jit(solution)/shard_map/jit(_take)/gather | solution.py:29
  46.6 0.0 copy-start.1
  46.6 0.1 compare_and_fusion
  46.7 0.0 copy-done
  46.7 1.7 %fusion.7 = f32[32,512]{0,1:T(8,128)S(1)} fusion(s32[1,6,512,256]{3,2,1,0:T(8,128)S(1)} %copy-done, s32[6]{0:T(128)S(1)} %fusion.20, bf16[32,6,256]{0,2,1:T(8,128)(2,1)} %bitcast.34, pred[6,256]{1,0:T(8,128)(4,1)S(1)} %compare_and_fusion), kind=kOutput, calls=%fused_computation.9 | convolution fusion | flops 51953664 | bytes 3311128 | tf_op jit(solution)/shard_map/fsk,sik->fi/dot_general | solution.py:33
  48.5 0.0 copy-done.1
  48.5 0.4 fusion.10
  48.9 0.1 copy.11
  49.0 5.4 %all_gather.11 = bf16[128,512]{1,0:T(8,128)(2,1)S(1)} all-gather(bf16[32,512]{1,0:T(8,128)(2,1)S(1)} %copy.11), channel_id=1, replica_groups=mesh['vert'=8,'af'=4] {'af'}, dimensions={0}, use_global_device_ids=true | all-gather | bytes 163840 | tf_op jit(solution)/shard_map/all_gather | solution.py:39
  54.4 0.0 copy-done.4
  54.4 5.2 %all_gather.9 = bf16[128,256]{1,0:T(8,128)(2,1)S(1)} all-gather(bf16[32,256]{1,0:T(8,128)(2,1)S(1)} %copy-done.4), channel_id=1, replica_groups=mesh['vert'=8,'af'=4] {'af'}, dimensions={0}, use_global_device_ids=true | all-gather | bytes 81920 | tf_op jit(solution)/shard_map/all_gather | solution.py:40
  59.6 0.0 copy-done.6
  59.6 0.9 %fusion.12 = bf16[64,512]{1,0:T(8,128)(2,1)} fusion(bf16[128,512]{1,0:T(8,128)(2,1)S(1)} %all_gather.11, f32[64]{0:T(128)S(1)} %copy-done.6, bf16[128,256]{1,0:T(8,128)(2,1)S(1)} %all_gather.9, s32[]{:T(128)S(6)} %select_n.25), kind=kOutput, calls=%fused_computation.13 | convolution fusion | flops 8486912 | bytes 229892 | tf_op jit(solution)/shard_map/dot_general | solution.py:44
  (5 shorter events, 0.1 us)
Async XLA Ops:
  0.0 41.4 %copy-start.7 = (s32[1,6]{1,0:T(1,128)S(1)}, s32[1,6]{1,0:T(1,128)}, u32[]{:S(2)}) copy-start(s32[1,6]{1,0:T(1,128)} %param.13) | copy-start | bytes 76
  0.0 4.5 %copy-start.5 = (s32[512]{0:T(512)S(1)}, s32[512]{0:T(512)}, u32[]{:S(2)}) copy-start(s32[512]{0:T(512)} %param.15) | copy-start | bytes 6148
  0.0 4.6 %copy-start.2 = (bf16[32,512]{1,0:T(8,128)(2,1)S(1)}, bf16[32,512]{1,0:T(8,128)(2,1)}, u32[]{:S(2)}) copy-start(bf16[32,512]{1,0:T(8,128)(2,1)} %param.8) | copy-start | bytes 98308
  0.0 41.5 %copy-start.3 = (s32[1,6,256]{2,0,1:T(1,128)S(1)}, s32[1,6,256]{2,0,1:T(1,128)}, u32[]{:S(2)}) copy-start(s32[1,6,256]{2,0,1:T(1,128)} %param.14) | copy-start | bytes 18436
  0.7 46.0 %copy-start = (s32[1,6,512,256]{3,2,1,0:T(8,128)S(1)}, s32[1,6,512,256]{3,2,1,0:T(8,128)}, u32[]{:S(2)}) copy-start(s32[1,6,512,256]{3,2,1,0:T(8,128)} %param.12) | copy-start | bytes 9437188
  41.6 12.8 %copy-start.4 = (bf16[32,256]{1,0:T(8,128)(2,1)S(1)}, bf16[32,256]{1,0:T(8,128)(2,1)}, u32[]{:S(2)}) copy-start(bf16[32,256]{1,0:T(8,128)(2,1)} %param.9) | copy-start | bytes 49156
  41.6 18.1 %copy-start.6 = (f32[64]{0:T(128)S(1)}, f32[64]{0:T(128)}, u32[]{:S(2)}) copy-start(f32[64]{0:T(128)} %param.10) | copy-start | bytes 772
  46.6 1.8 %copy-start.1 = (s32[1,512,512]{2,1,0:T(8,128)S(1)}, s32[1,512,512]{2,1,0:T(8,128)}, u32[]{:S(2)}) copy-start(s32[1,512,512]{2,1,0:T(8,128)} %param.11) | copy-start | bytes 3145732
where the time goes:
time: 60.8 us; the launch traced here: 60.5 us
  blocking collectives  47.2 us (78%)
  local copies, waits for them, and re-layouts  5.35 us (9%)
  other arithmetic  4.78 us (8%)
  matrix products  3.06 us (5%)
    all_gather x1, blocking collectives, body(): gathered = lax.all_gather(scaled, 'vert', axis=1, tiled=True)  36.6 us
    all_gather x1, blocking collectives, body(): lax.all_gather(aggregated, 'af', axis=0, tiled=True)  5.42 us
    all_gather x1, blocking collectives, body(): lax.all_gather(weight, 'af', axis=0, tiled=True)  5.22 us
    gather x1, local copies, waits for them, and re-layouts, body(): jnp.take(gathered, column_ids.reshape(-1), axis=1)  5.03 us
    reduce_sum x1, other arithmetic, body(): jnp.sum(jnp.sum(live_blocks, axis=-1), axis=0)  2.42 us
    dot_general x1, matrix products, body(): jnp.einsum('fsk,sik->fi', halo_vals, halo_blocks, preferred_element_type=...  1.75 us
    reduce_sum x1, other arithmetic, body(): jnp.sum(self_mask[0], axis=-1)  1.37 us

commit v1 on v0

v1 whole, which is shorter than its diff:
```python
import functools

import jax
import jax.numpy as jnp
from jax import lax
from jax.experimental import pallas as pl
from jax.experimental.pallas import tpu as pltpu
from jax.sharding import PartitionSpec as P

MESH = pl.DeviceIdType.MESH
LANES = 128
NT = (((1,), (1,)), ((), ()))
NN = (((1,), (0,)), ((), ()))


def lane_gather(table, index):
    parts = []
    for start in range(0, index.shape[1], LANES):
        wanted = index[:, start : start + LANES]
        low, high = wanted % LANES, wanted // LANES
        picked = jnp.zeros(wanted.shape, table.dtype)
        for piece in range(table.shape[1] // LANES):
            seen = jnp.take_along_axis(
                table[:, piece * LANES : (piece + 1) * LANES], low, axis=1, mode="promise_in_bounds"
            )
            picked = jnp.where(high == piece, seen, picked)
        parts.append(picked)
    return jnp.concatenate(parts, axis=1)


def kernel(
    n_vert, n_af, n_chunk,
    feat, weight, bias, self_mask, halo_mask, sources, rows, outside,
    out,
    feat_all, weight_all, bias_v, self_v, halo_v, source_s, rows_v, outside_v,
    root_all, agg_all, self_b, halo_b, weight_t, root_pick,
    small_sem, self_sem, halo_sem,
    feat_send, feat_recv, weight_send, weight_recv, root_send, root_recv, agg_send, agg_recv,
):
    my_vert, my_af = lax.axis_index("vert"), lax.axis_index("af")
    n_slot, block, halo = halo_v.shape
    span = block // n_chunk

    small = [
        pltpu.make_async_copy(src, dst, small_sem.at[i])
        for i, (src, dst) in enumerate((
            (sources, source_s),
            (outside, outside_v),
            (feat, feat_all.at[my_vert]),
            (rows, rows_v),
            (weight, weight_all.at[my_af]),
            (bias, bias_v),
        ))
    ]
    own_copies, halo_copies = [], []
    small[0].start()
    for c in range(n_chunk):
        part = pl.ds(c * span, span)
        halo_copies.append(
            pltpu.make_async_copy(halo_mask.at[:, part, :], halo_v.at[:, part, :], halo_sem.at[c])
        )
        own_copies.append(pltpu.make_async_copy(self_mask.at[part, :], self_v.at[part, :], self_sem.at[c]))
        halo_copies[c].start()
        own_copies[c].start()
    for copy in small[1:]:
        copy.start()

    barrier = pltpu.get_barrier_semaphore()
    for k in range(1, n_vert):
        pl.semaphore_signal(barrier, inc=1, device_id={"vert": lax.rem(my_vert + k, n_vert)}, device_id_type=MESH)
    for k in range(1, n_af):
        pl.semaphore_signal(barrier, inc=1, device_id={"af": lax.rem(my_af + k, n_af)}, device_id_type=MESH)
    pl.semaphore_wait(barrier, n_vert + n_af - 2)

    def to_vert(src, dst, send, recv):
        copies = [
            pltpu.make_async_remote_copy(
                src_ref=src, dst_ref=dst, send_sem=send.at[k], recv_sem=recv.at[k],
                device_id={"vert": lax.rem(my_vert + k, n_vert)}, device_id_type=MESH,
            )
            for k in range(1, n_vert)
        ]
        for copy in copies:
            copy.start()
        return copies

    def to_af(src, dst, send, recv):
        copies = [
            pltpu.make_async_remote_copy(
                src_ref=src, dst_ref=dst, send_sem=send.at[k], recv_sem=recv.at[k],
                device_id={"af": lax.rem(my_af + k, n_af)}, device_id_type=MESH,
            )
            for k in range(1, n_af)
        ]
        for copy in copies:
            copy.start()
        return copies

    feat_copies = to_vert(feat, feat_all.at[my_vert], feat_send, feat_recv)
    weight_copies = to_af(weight, weight_all.at[my_af], weight_send, weight_recv)

    small[0].wait()
    small[1].wait()
    source = [source_s[0, s] for s in range(n_slot)]
    live = [jnp.where(src >= 0, 1.0, 0.0).astype(jnp.float32) for src in source]
    source = [jnp.maximum(src, 0) for src in source]
    ones = jnp.ones((8, halo), jnp.bfloat16)
    for c in range(n_chunk):
        part = pl.ds(c * span, span)
        halo_copies[c].wait()
        own_copies[c].wait()
        count = jnp.zeros((span, halo), jnp.bfloat16)
        for j in range(0, block, halo):
            entries = self_v[part, j : j + halo].astype(jnp.float32).astype(jnp.bfloat16)
            self_b[part, j : j + halo] = entries
            count = count + entries
        for s in range(n_slot):
            entries = (halo_v[s, part, :].astype(jnp.float32) * live[s]).astype(jnp.bfloat16)
            halo_b[part, s * halo : (s + 1) * halo] = entries
            count = count + entries
        edges = lax.dot_general(ones, count, NT, preferred_element_type=jnp.float32)[0:1]
        degree = 1.0 + edges + outside_v[:, part].astype(jnp.float32)
        root_all[my_vert, :, part] = 1.0 / jnp.sqrt(degree)
    root_copies = to_vert(root_all.at[my_vert], root_all.at[my_vert], root_send, root_recv)

    root = root_all[my_vert]
    small[2].wait()
    scaled = (feat_all[my_vert].astype(jnp.float32) * root).astype(jnp.bfloat16)
    summed = scaled.astype(jnp.float32) + lax.dot_general(scaled, self_b[...], NT, preferred_element_type=jnp.float32)

    small[3].wait()
    index = jnp.concatenate([rows_v[...], jnp.zeros((8 - n_slot, halo), jnp.int32)], axis=0)
    for copy in feat_copies:
        copy.wait_recv()
    column = lax.broadcasted_iota(jnp.int32, (block, halo), 0)
    picked = []
    for s in range(n_slot):
        chosen = (column == rows_v[s : s + 1, :]).astype(jnp.float32).astype(jnp.bfloat16)
        picked.append(
            lax.dot_general(feat_all[source[s]], chosen, NN, preferred_element_type=jnp.float32)
        )

    small[4].wait()
    small[5].wait()
    for copy in weight_copies:
        copy.wait_recv()
    f_in = weight_all.shape[0] * weight_all.shape[1]
    whole = weight_all[...].astype(jnp.float32).reshape(f_in, weight_all.shape[2])
    weight_t[...] = whole.T.astype(jnp.bfloat16)
    out_rows = out.shape[0]
    weight_cols = weight_t[pl.ds(pl.multiple_of(my_af * out_rows, out_rows), out_rows), :]
    square = (out_rows, out_rows)
    diagonal = lax.broadcasted_iota(jnp.int32, square, 0) == lax.broadcasted_iota(jnp.int32, square, 1)
    offset = jnp.sum(jnp.where(diagonal, jnp.broadcast_to(bias_v[...], square), 0.0), axis=1, keepdims=True)

    for copy in root_copies:
        copy.wait_recv()
    root_pick[...] = jnp.zeros_like(root_pick)
    for s in range(n_slot):
        root_pick[s : s + 1, :] = root_all[source[s]]
    roots = lane_gather(root_pick[...], index)
    values = jnp.concatenate(
        [(picked[s] * roots[s : s + 1, :]).astype(jnp.bfloat16) for s in range(n_slot)], axis=1
    )
    summed = summed + lax.dot_general(values, halo_b[...], NT, preferred_element_type=jnp.float32)
    agg_all[my_af] = (summed * root).astype(jnp.bfloat16)
    agg_copies = to_af(agg_all.at[my_af], agg_all.at[my_af], agg_send, agg_recv)
    for copy in feat_copies + weight_copies + root_copies:
        copy.wait_send()
    for copy in agg_copies:
        copy.wait_recv()
    mixed = lax.dot_general(
        weight_cols, agg_all[...].reshape(f_in, block), NN, preferred_element_type=jnp.float32
    )
    out[...] = jnp.maximum(mixed + offset, 0.0).astype(jnp.bfloat16)
    for copy in agg_copies:
        copy.wait_send()


def solution(mesh):
    n_vert, n_af = mesh.shape["vert"], mesh.shape["af"]

    def body(features_t, weight, bias, self_mask, halo_mask, block_src, halo_rows, outside_degree):
        feat_count, block = features_t.shape
        n_slot, halo = halo_rows.shape[1:]
        out_rows = bias.shape[0]
        n_chunk = 4
        anywhere = pl.BlockSpec(memory_space=pl.ANY)
        return pl.pallas_call(
            functools.partial(kernel, n_vert, n_af, n_chunk),
            out_shape=jax.ShapeDtypeStruct((out_rows, block), jnp.bfloat16),
            in_specs=[anywhere] * 8,
            out_specs=pl.BlockSpec(memory_space=pltpu.VMEM),
            scratch_shapes=[
                pltpu.VMEM((n_vert, feat_count, block), jnp.bfloat16),
                pltpu.VMEM((n_af,) + weight.shape, jnp.bfloat16),
                pltpu.VMEM((1, out_rows), jnp.float32),
                pltpu.VMEM((block, block), jnp.int32),
                pltpu.VMEM((n_slot, block, halo), jnp.int32),
                pltpu.SMEM((1, n_slot), jnp.int32),
                pltpu.VMEM((n_slot, halo), jnp.int32),
                pltpu.VMEM((1, block), jnp.int32),
                pltpu.VMEM((n_vert, 1, block), jnp.float32),
                pltpu.VMEM((n_af, feat_count, block), jnp.bfloat16),
                pltpu.VMEM((block, block), jnp.bfloat16),
                pltpu.VMEM((block, n_slot * halo), jnp.bfloat16),
                pltpu.VMEM((weight.shape[1], n_af * feat_count), jnp.bfloat16),
                pltpu.VMEM((8, block), jnp.float32),
                pltpu.SemaphoreType.DMA((6,)),
                pltpu.SemaphoreType.DMA((n_chunk,)),
                pltpu.SemaphoreType.DMA((n_chunk,)),
                pltpu.SemaphoreType.DMA((n_vert,)),
                pltpu.SemaphoreType.DMA((n_vert,)),
                pltpu.SemaphoreType.DMA((n_af,)),
                pltpu.SemaphoreType.DMA((n_af,)),
                pltpu.SemaphoreType.DMA((n_vert,)),
                pltpu.SemaphoreType.DMA((n_vert,)),
                pltpu.SemaphoreType.DMA((n_af,)),
                pltpu.SemaphoreType.DMA((n_af,)),
            ],
            compiler_params=pltpu.CompilerParams(collective_id=0, has_side_effects=True),
        )(
            features_t, weight, bias.reshape(1, -1), self_mask[0], halo_mask[0], block_src,
            halo_rows[0], outside_degree.reshape(1, -1),
        )

    return jax.shard_map(
        body,
        mesh=mesh,
        in_specs=(
            P("af", "vert"),
            P("af", None),
            P("af"),
            P("vert", None, None),
            P("vert", None, None, None),
            P("vert", None),
            P("vert", None, None),
            P("vert"),
        ),
        out_specs=P("af", "vert"),
        check_vma=False,
    )
```

time: 60.8 us -> 21.5 us (0.35)
  blocking collectives: 47.2 us -> 0 us
  Pallas kernels: 0 us -> 18.6 us
  other arithmetic: 4.78 us -> 0 us
  matrix products: 3.06 us -> 0 us
  local copies, waits for them, and re-layouts: 5.35 us -> 2.76 us
    all_gather x3 -> x0, blocking collectives: 47.2 us -> none  [the longest x1 36.6 us: body(): gathered = lax.all_gather(scaled, 'vert', axis=1, tiled=True)]
    pallas_call x0 -> x1, Pallas kernels: none -> 18.6 us  [body(): pl.pallas_call(functools.partial(kernel, n_vert, n_af, n_chunk), out_shap...]
    gather x1 -> x0, local copies, waits for them, and re-layouts: 5.03 us -> none  [body(): jnp.take(gathered, column_ids.reshape(-1), axis=1)]
    reduce_sum x2 -> x0, other arithmetic: 3.8 us -> none  [the longest x1 2.42 us: body(): jnp.sum(jnp.sum(live_blocks, axis=-1), axis=0)]
    dot_general x3 -> x0, matrix products: 3.06 us -> none  [the longest x1 1.75 us: body(): jnp.einsum('fsk,sik->fi', halo_vals, halo_blocks, preferred_element_type=...]
    unnamed x19 -> x2, local copies, waits for them, and re-layouts: 0.24 us -> 2.76 us
    convert_element_type x2 -> x0, other arithmetic: 0.86 us -> none  [the longest x1 0.72 us: body(): live_blocks = halo_mask[0] * live_slot.astype(jnp.int32)[:, None, None]]
where the time goes in v1:
time: 21.5 us; the launch traced here: 21.3 us
  Pallas kernels  18.6 us (87%)
  local copies, waits for them, and re-layouts  2.76 us (13%)
    pallas_call x1, Pallas kernels, body(): pl.pallas_call(functools.partial(kernel, n_vert, n_af, n_chunk), out_shap...  18.6 us
    unnamed x2, local copies, waits for them, and re-layouts  2.76 us

profile of v1, /device:TPU:0, one launch (start us, length us, event | category | flops | bytes accessed | tf_op | source)
XLA Modules:
  0.0 21.3 jit_solution(17321759165209866369)
XLA Ops:
  0.0 1.3 %copy.11 = s32[1,6,256]{2,1,0:T(8,128)} copy(s32[1,6,256]{2,0,1:T(1,128)} %param.14) | data formatting | bytes 12288
  1.3 18.6 %shard_map.82 = bf16[64,512]{1,0:T(8,128)(2,1)} custom-call(bf16[32,512]{1,0:T(8,128)(2,1)} %feat.1, bf16[32,256]{1,0:T(8,128)(2,1)} %weight.1, f32[1,64]{1,0:T(1,128)} %bitcast.11, s32[512,512]{1,0:T(8,128)} %bitcast.8, s32[6,512,256]{2,1,0:T(8,128)} %bitcast.7, s32[1,6]{1,0:T(1,128)} %sources.1, s32[6,256]{1,0:T(8,128)} %bitcast.9, s32[1,512]{1,0:T(1,128)} %bitcast.10), custom_call_target="tpu_custom_call" | custom-call | tf_op jit(solution)/shard_map/pallas_call | solution.py:189
  19.9 1.5 %copy.13 = bf16[64,512]{1,0:T(8,128)(2,1)} copy(bf16[64,512]{1,0:T(8,128)(2,1)} %shard_map.82) | data formatting | bytes 131072

commit v2 on v1

--- a/solution.py
+++ b/solution.py
@@ -33,7 +33,7 @@
     feat, weight, bias, self_mask, halo_mask, sources, rows, outside,
     out,
     feat_all, weight_all, bias_v, self_v, halo_v, source_s, rows_v, outside_v,
-    root_all, agg_all, self_b, halo_b, weight_t, root_pick,
+    root_all, agg_all, self_b, halo_b, weight_t, root_pick, row_pick,
     small_sem, self_sem, halo_sem,
     feat_send, feat_recv, weight_send, weight_recv, root_send, root_recv, agg_send, agg_recv,
 ):
@@ -53,6 +53,7 @@
         ))
     ]
     own_copies, halo_copies = [], []
+    small[2].start()
     small[0].start()
     for c in range(n_chunk):
         part = pl.ds(c * span, span)
@@ -62,8 +63,8 @@
         own_copies.append(pltpu.make_async_copy(self_mask.at[part, :], self_v.at[part, :], self_sem.at[c]))
         halo_copies[c].start()
         own_copies[c].start()
-    for copy in small[1:]:
-        copy.start()
+    for i in (1, 3, 4, 5):
+        small[i].start()
 
     barrier = pltpu.get_barrier_semaphore()
     for k in range(1, n_vert):
@@ -96,7 +97,8 @@
             copy.start()
         return copies
 
-    feat_copies = to_vert(feat, feat_all.at[my_vert], feat_send, feat_recv)
+    small[2].wait()
+    feat_copies = to_vert(feat_all.at[my_vert], feat_all.at[my_vert], feat_send, feat_recv)
     weight_copies = to_af(weight, weight_all.at[my_af], weight_send, weight_recv)
 
     small[0].wait()
@@ -124,18 +126,20 @@
     root_copies = to_vert(root_all.at[my_vert], root_all.at[my_vert], root_send, root_recv)
 
     root = root_all[my_vert]
-    small[2].wait()
     scaled = (feat_all[my_vert].astype(jnp.float32) * root).astype(jnp.bfloat16)
     summed = scaled.astype(jnp.float32) + lax.dot_general(scaled, self_b[...], NT, preferred_element_type=jnp.float32)
 
     small[3].wait()
-    index = jnp.concatenate([rows_v[...], jnp.zeros((8 - n_slot, halo), jnp.int32)], axis=0)
+    row_pick[...] = jnp.zeros_like(row_pick)
+    for s in range(n_slot):
+        row_pick[s : s + 1, :] = rows_v[s]
+    index = row_pick[...]
     for copy in feat_copies:
         copy.wait_recv()
     column = lax.broadcasted_iota(jnp.int32, (block, halo), 0)
     picked = []
     for s in range(n_slot):
-        chosen = (column == rows_v[s : s + 1, :]).astype(jnp.float32).astype(jnp.bfloat16)
+        chosen = (column == rows_v[s]).astype(jnp.float32).astype(jnp.bfloat16)
         picked.append(
             lax.dot_general(feat_all[source[s]], chosen, NN, preferred_element_type=jnp.float32)
         )
@@ -162,18 +166,26 @@
     values = jnp.concatenate(
         [(picked[s] * roots[s : s + 1, :]).astype(jnp.bfloat16) for s in range(n_slot)], axis=1
     )
-    summed = summed + lax.dot_general(values, halo_b[...], NT, preferred_element_type=jnp.float32)
-    agg_all[my_af] = (summed * root).astype(jnp.bfloat16)
-    agg_copies = to_af(agg_all.at[my_af], agg_all.at[my_af], agg_send, agg_recv)
+    halves = []
+    for h in range(2):
+        part = pl.ds(h * (block // 2), block // 2)
+        total = summed[:, h * (block // 2) : (h + 1) * (block // 2)] + lax.dot_general(
+            values, halo_b[part, :], NT, preferred_element_type=jnp.float32
+        )
+        agg_all[my_af, :, part] = (total * root_all[my_vert, :, part]).astype(jnp.bfloat16)
+        sent = agg_all.at[my_af, :, part]
+        halves.append(to_af(sent, sent, agg_send.at[h], agg_recv.at[h]))
     for copy in feat_copies + weight_copies + root_copies:
         copy.wait_send()
-    for copy in agg_copies:
-        copy.wait_recv()
-    mixed = lax.dot_general(
-        weight_cols, agg_all[...].reshape(f_in, block), NN, preferred_element_type=jnp.float32
-    )
-    out[...] = jnp.maximum(mixed + offset, 0.0).astype(jnp.bfloat16)
-    for copy in agg_copies:
+    for h in range(2):
+        part = pl.ds(h * (block // 2), block // 2)
+        for copy in halves[h]:
+            copy.wait_recv()
+        mixed = lax.dot_general(
+            weight_cols, agg_all[:, :, part].reshape(f_in, block // 2), NN, preferred_element_type=jnp.float32
+        )
+        out[:, part] = (mixed + offset).astype(jnp.bfloat16)
+    for copy in halves[0] + halves[1]:
         copy.wait_send()
 
 
@@ -185,8 +197,8 @@
         n_slot, halo = halo_rows.shape[1:]
         out_rows = bias.shape[0]
         n_chunk = 4
-        anywhere = pl.BlockSpec(memory_space=pl.ANY)
-        return pl.pallas_call(
+        anywhere = pl.BlockSpec(memory_space=pltpu.HBM)
+        mixed = pl.pallas_call(
             functools.partial(kernel, n_vert, n_af, n_chunk),
             out_shape=jax.ShapeDtypeStruct((out_rows, block), jnp.bfloat16),
             in_specs=[anywhere] * 8,
@@ -198,7 +210,7 @@
                 pltpu.VMEM((block, block), jnp.int32),
                 pltpu.VMEM((n_slot, block, halo), jnp.int32),
                 pltpu.SMEM((1, n_slot), jnp.int32),
-                pltpu.VMEM((n_slot, halo), jnp.int32),
+                pltpu.VMEM((n_slot, 1, halo), jnp.int32),
                 pltpu.VMEM((1, block), jnp.int32),
                 pltpu.VMEM((n_vert, 1, block), jnp.float32),
                 pltpu.VMEM((n_af, feat_count, block), jnp.bfloat16),
@@ -206,6 +218,7 @@
                 pltpu.VMEM((block, n_slot * halo), jnp.bfloat16),
                 pltpu.VMEM((weight.shape[1], n_af * feat_count), jnp.bfloat16),
                 pltpu.VMEM((8, block), jnp.float32),
+                pltpu.VMEM((8, halo), jnp.int32),
                 pltpu.SemaphoreType.DMA((6,)),
                 pltpu.SemaphoreType.DMA((n_chunk,)),
                 pltpu.SemaphoreType.DMA((n_chunk,)),
@@ -215,14 +228,20 @@
                 pltpu.SemaphoreType.DMA((n_af,)),
                 pltpu.SemaphoreType.DMA((n_vert,)),
                 pltpu.SemaphoreType.DMA((n_vert,)),
-                pltpu.SemaphoreType.DMA((n_af,)),
-                pltpu.SemaphoreType.DMA((n_af,)),
+                pltpu.SemaphoreType.DMA((2, n_af)),
+                pltpu.SemaphoreType.DMA((2, n_af)),
             ],
-            compiler_params=pltpu.CompilerParams(collective_id=0, has_side_effects=True),
-        )(
-            features_t, weight, bias.reshape(1, -1), self_mask[0], halo_mask[0], block_src,
-            halo_rows[0], outside_degree.reshape(1, -1),
-        )
+            compiler_params=pltpu.CompilerParams(
+                collective_id=0, has_side_effects=True, vmem_limit_bytes=24 * 1024 * 1024
+            ),
+        )(*(
+            pltpu.with_memory_space_constraint(each, pltpu.HBM)
+            for each in (
+                features_t, weight, bias.reshape(1, -1), self_mask[0], halo_mask[0], block_src,
+                jnp.swapaxes(halo_rows, 0, 1), outside_degree.reshape(1, -1),
+            )
+        ))
+        return jnp.maximum(mixed, 0)
 
     return jax.shard_map(
         body,

time: 21.5 us -> 18.7 us (0.87)
  local copies, waits for them, and re-layouts: 2.76 us -> 0 us
  Pallas kernels: 18.6 us -> 17.9 us
  other arithmetic: 0 us -> 0.64 us
    unnamed x2 -> x0, local copies, waits for them, and re-layouts: 2.76 us -> none
    pallas_call x1, Pallas kernels: 18.6 us -> 17.9 us  [body(): pl.pallas_call(functools.partial(kernel, n_vert, n_af, n_chunk), out_shap...]
    max x0 -> x1, other arithmetic: none -> 0.64 us  [body(): return jnp.maximum(mixed, 0)]
where the time goes in v2:
time: 18.7 us; the launch traced here: 18.5 us
  Pallas kernels  17.9 us (96%)
  other arithmetic  0.64 us (3%)
    pallas_call x1, Pallas kernels, body(): pl.pallas_call(functools.partial(kernel, n_vert, n_af, n_chunk), out_shap...  17.9 us
    max x1, other arithmetic, body(): return jnp.maximum(mixed, 0)  0.64 us

profile of v2, /device:TPU:0, one launch (start us, length us, event | category | flops | bytes accessed | tf_op | source)
XLA Modules:
  0.0 18.5 jit_solution(11628509492839642446)
XLA Ops:
  0.0 17.9 %shard_map.82 = bf16[64,512]{1,0:T(8,128)(2,1)S(1)} custom-call(bf16[32,512]{1,0:T(8,128)(2,1)} %feat.1, bf16[32,256]{1,0:T(8,128)(2,1)} %weight.1, f32[1,64]{1,0:T(1,128)} %bitcast.9, s32[512,512]{1,0:T(8,128)} %bitcast.6, s32[6,512,256]{2,1,0:T(8,128)} %bitcast.5, s32[1,6]{1,0:T(1,128)} %sources.1, s32[6,1,256]{2,1,0:T(1,128)} %bitcast.7, s32[1,512]{1,0:T(1,128)} %bitcast.8), custom_call_target="tpu_custom_call" | custom-call | tf_op jit(solution)/shard_map/pallas_call | solution.py:201
  17.9 0.6 %broadcast_maximum_fusion = bf16[64,512]{1,0:T(8,128)(2,1)} fusion(bf16[64,512]{1,0:T(8,128)(2,1)S(1)} %shard_map.82), kind=kLoop, calls=%fused_computation | loop fusion | flops 32768 | bytes 131072 | tf_op jit(solution)/shard_map/max | solution.py:244

commit v3 on v2

--- a/solution.py
+++ b/solution.py
@@ -33,13 +33,19 @@
     feat, weight, bias, self_mask, halo_mask, sources, rows, outside,
     out,
     feat_all, weight_all, bias_v, self_v, halo_v, source_s, rows_v, outside_v,
-    root_all, agg_all, self_b, halo_b, weight_t, root_pick, row_pick,
+    root_all, agg_all, self_b, halo_b, weight_t, root_pick, row_pick, chosen, halo_t,
     small_sem, self_sem, halo_sem,
     feat_send, feat_recv, weight_send, weight_recv, root_send, root_recv, agg_send, agg_recv,
 ):
     my_vert, my_af = lax.axis_index("vert"), lax.axis_index("af")
     n_slot, block, halo = halo_v.shape
     span = block // n_chunk
+
+    barrier = pltpu.get_barrier_semaphore()
+    for k in range(1, n_vert):
+        pl.semaphore_signal(barrier, inc=1, device_id={"vert": lax.rem(my_vert + k, n_vert)}, device_id_type=MESH)
+    for k in range(1, n_af):
+        pl.semaphore_signal(barrier, inc=1, device_id={"af": lax.rem(my_af + k, n_af)}, device_id_type=MESH)
 
     small = [
         pltpu.make_async_copy(src, dst, small_sem.at[i])
@@ -66,11 +72,6 @@
     for i in (1, 3, 4, 5):
         small[i].start()
 
-    barrier = pltpu.get_barrier_semaphore()
-    for k in range(1, n_vert):
-        pl.semaphore_signal(barrier, inc=1, device_id={"vert": lax.rem(my_vert + k, n_vert)}, device_id_type=MESH)
-    for k in range(1, n_af):
-        pl.semaphore_signal(barrier, inc=1, device_id={"af": lax.rem(my_af + k, n_af)}, device_id_type=MESH)
     pl.semaphore_wait(barrier, n_vert + n_af - 2)
 
     def to_vert(src, dst, send, recv):
@@ -98,7 +99,29 @@
         return copies
 
     small[2].wait()
-    feat_copies = to_vert(feat_all.at[my_vert], feat_all.at[my_vert], feat_send, feat_recv)
+    group = n_vert // 2 if n_vert % 2 == 0 else n_vert
+    n_step = 2 if group < n_vert else 0
+    depth = feat.shape[0] // max(n_step, 1)
+    base, place = my_vert // group * group, lax.rem(my_vert, group)
+    partner = lax.rem(my_vert + group, n_vert)
+
+    def feature_copy(ref, i, target):
+        return pltpu.make_async_remote_copy(
+            src_ref=ref, dst_ref=ref, send_sem=feat_send.at[i], recv_sem=feat_recv.at[i],
+            device_id={"vert": target}, device_id_type=MESH,
+        )
+
+    def near(j):
+        return base + lax.rem(place + j, group)
+
+    across = [
+        feature_copy(feat_all.at[my_vert, pl.ds(h * depth, depth), :], h, partner) for h in range(n_step)
+    ]
+    feat_copies = across + [
+        feature_copy(feat_all.at[my_vert], n_step + j, near(j)) for j in range(1, group)
+    ]
+    for copy in feat_copies:
+        copy.start()
     weight_copies = to_af(weight, weight_all.at[my_af], weight_send, weight_recv)
 
     small[0].wait()
@@ -125,6 +148,15 @@
         root_all[my_vert, :, part] = 1.0 / jnp.sqrt(degree)
     root_copies = to_vert(root_all.at[my_vert], root_all.at[my_vert], root_send, root_recv)
 
+    for h in range(n_step):
+        across[h].wait_recv()
+        for j in range(1, group):
+            passed = feature_copy(
+                feat_all.at[partner, pl.ds(h * depth, depth), :], n_step + (h + 1) * group + j, near(j)
+            )
+            passed.start()
+            feat_copies.append(passed)
+
     root = root_all[my_vert]
     scaled = (feat_all[my_vert].astype(jnp.float32) * root).astype(jnp.bfloat16)
     summed = scaled.astype(jnp.float32) + lax.dot_general(scaled, self_b[...], NT, preferred_element_type=jnp.float32)
@@ -134,15 +166,9 @@
     for s in range(n_slot):
         row_pick[s : s + 1, :] = rows_v[s]
     index = row_pick[...]
-    for copy in feat_copies:
-        copy.wait_recv()
     column = lax.broadcasted_iota(jnp.int32, (block, halo), 0)
-    picked = []
     for s in range(n_slot):
-        chosen = (column == rows_v[s]).astype(jnp.float32).astype(jnp.bfloat16)
-        picked.append(
-            lax.dot_general(feat_all[source[s]], chosen, NN, preferred_element_type=jnp.float32)
-        )
+        chosen[s] = (column == rows_v[s]).astype(jnp.float32).astype(jnp.bfloat16)
 
     small[4].wait()
     small[5].wait()
@@ -156,6 +182,14 @@
     square = (out_rows, out_rows)
     diagonal = lax.broadcasted_iota(jnp.int32, square, 0) == lax.broadcasted_iota(jnp.int32, square, 1)
     offset = jnp.sum(jnp.where(diagonal, jnp.broadcast_to(bias_v[...], square), 0.0), axis=1, keepdims=True)
+
+    halo_t[...] = halo_b[...].T
+    for copy in feat_copies[n_step:]:
+        copy.wait_recv()
+    picked = [
+        lax.dot_general(feat_all[source[s]], chosen[s], NN, preferred_element_type=jnp.float32)
+        for s in range(n_slot)
+    ]
 
     for copy in root_copies:
         copy.wait_recv()
@@ -170,7 +204,7 @@
     for h in range(2):
         part = pl.ds(h * (block // 2), block // 2)
         total = summed[:, h * (block // 2) : (h + 1) * (block // 2)] + lax.dot_general(
-            values, halo_b[part, :], NT, preferred_element_type=jnp.float32
+            values, halo_t[:, part], NN, preferred_element_type=jnp.float32
         )
         agg_all[my_af, :, part] = (total * root_all[my_vert, :, part]).astype(jnp.bfloat16)
         sent = agg_all.at[my_af, :, part]
@@ -219,11 +253,13 @@
                 pltpu.VMEM((weight.shape[1], n_af * feat_count), jnp.bfloat16),
                 pltpu.VMEM((8, block), jnp.float32),
                 pltpu.VMEM((8, halo), jnp.int32),
+                pltpu.VMEM((n_slot, block, halo), jnp.bfloat16),
+                pltpu.VMEM((n_slot * halo, block), jnp.bfloat16),
                 pltpu.SemaphoreType.DMA((6,)),
                 pltpu.SemaphoreType.DMA((n_chunk,)),
                 pltpu.SemaphoreType.DMA((n_chunk,)),
-                pltpu.SemaphoreType.DMA((n_vert,)),
-                pltpu.SemaphoreType.DMA((n_vert,)),
+                pltpu.SemaphoreType.DMA((2 * n_vert + 2,)),
+                pltpu.SemaphoreType.DMA((2 * n_vert + 2,)),
                 pltpu.SemaphoreType.DMA((n_af,)),
                 pltpu.SemaphoreType.DMA((n_af,)),
                 pltpu.SemaphoreType.DMA((n_vert,)),

time: 18.7 us -> 17.5 us (0.936)
  Pallas kernels: 17.9 us -> 16.7 us
    pallas_call x1, Pallas kernels: 17.9 us -> 16.7 us  [body(): pl.pallas_call(functools.partial(kernel, n_vert, n_af, n_chunk), out_shap...]
where the time goes in v3:
time: 17.5 us; the launch traced here: 17.3 us
  Pallas kernels  16.7 us (95%)
  other arithmetic  0.64 us (4%)
    pallas_call x1, Pallas kernels, body(): pl.pallas_call(functools.partial(kernel, n_vert, n_af, n_chunk), out_shap...  16.7 us
    max x1, other arithmetic, body(): return jnp.maximum(mixed, 0)  0.64 us

profile of v3, /device:TPU:0, one launch (start us, length us, event | category | flops | bytes accessed | tf_op | source)
XLA Modules:
  0.0 17.3 jit_solution(2051125099328218343)
XLA Ops:
  0.0 16.7 %shard_map.82 = bf16[64,512]{1,0:T(8,128)(2,1)S(1)} custom-call(bf16[32,512]{1,0:T(8,128)(2,1)} %feat.1, bf16[32,256]{1,0:T(8,128)(2,1)} %weight.1, f32[1,64]{1,0:T(1,128)} %bitcast.9, s32[512,512]{1,0:T(8,128)} %bitcast.6, s32[6,512,256]{2,1,0:T(8,128)} %bitcast.5, s32[1,6]{1,0:T(1,128)} %sources.1, s32[6,1,256]{2,1,0:T(1,128)} %bitcast.7, s32[1,512]{1,0:T(1,128)} %bitcast.8), custom_call_target="tpu_custom_call" | custom-call | tf_op jit(solution)/shard_map/pallas_call | solution.py:235
  16.7 0.6 %broadcast_maximum_fusion = bf16[64,512]{1,0:T(8,128)(2,1)} fusion(bf16[64,512]{1,0:T(8,128)(2,1)S(1)} %shard_map.82), kind=kLoop, calls=%fused_computation | loop fusion | flops 32768 | bytes 131072 | tf_op jit(solution)/shard_map/max | solution.py:280
